TPU v7x, 32 devices: a whole 2x2x4 slice. The times are simulated.
32 devices in a mesh: section: 4 (over y, x), dp: 8 (over z, core).
Axes of the slice: x: 2, y: 2, z: 4, core: 2. Of those that a mesh axis runs over, the one named last changes fastest.
Arguments:
- activations: bfloat16 [4, 8, 257, 1792], P('section', 'dp'), may hold values from -6 to 6
- saved: bfloat16 [4, 8, 257, 1792], P('section', 'dp'), may hold values from -6 to 6
- cotangents: bfloat16 [4, 8, 257, 1792], P('section', 'dp'), may hold values from -1.1953125 to 1.1953125
- projection: bfloat16 [4, 1792, 1792], P('section'), may hold values from -0.125 to 0.125
- section_gain: float32 [4, 1792], P('section'), may hold values from 0.5 to 1.5
- final_gain: float32 [1792], replicated, may hold values from 0.5 to 1.5
- head_weight: bfloat16 [1792, 1024], P('section'), may hold values from -0.125 to 0.125
- text_embed: bfloat16 [8, 1024], P('dp'), may hold values from -6 to 6
- labels: int32 [8], P('dp'), may hold values from 0 to 7, each once
Outputs:
- next_act: bfloat16 [4, 8, 257, 1792], P('section', 'dp')
- next_grad: bfloat16 [4, 8, 257, 1792], P('section', 'dp')
- mean_loss: float32 [4], P('section')
Inputs may be any that keep to these rules, and one draw needn't show every extreme that they name: labels holds each caption index once.
All inputs are finite; a program needn't handle non-finite values.
Results may differ from a plain program's by a relative error of at most 0.0039.
Values may be sent and summed in bfloat16 or wider, within the bound.
A program may use at most 64 MiB of HBM per device.

v0:
```python
import jax
import jax.numpy as jnp
from jax import lax
from jax.sharding import PartitionSpec as P

epsilon = 1e-06
logit_scale = 100.0


def shifted(value, axis, steps):
    count = lax.axis_size(axis)
    first, last = (max(0, -steps), min(count, count - steps))
    return lax.ppermute(value, axis, [(source, source + steps) for source in range(first, last)])


def spread(block, axis, owner):
    block = jnp.where(lax.axis_index(axis) == owner, block, jnp.zeros_like(block))
    return lax.psum(block, axis)


def norm_rows(values):
    centre = jnp.mean(values, axis=-1, keepdims=True)
    centred = values - centre
    variance = jnp.mean(centred * centred, axis=-1, keepdims=True)
    inverse = lax.rsqrt(variance + epsilon)
    return (centred * inverse, inverse)


def unit_rows(values):
    inverse = lax.rsqrt(jnp.sum(values * values, axis=-1, keepdims=True) + epsilon)
    return (values * inverse, inverse)


def forward_block(block_in, weight, scale_row):
    block_shape = block_in.shape
    standard, inverse = norm_rows(block_in.astype(jnp.float32))
    normed = (standard * scale_row).astype(jnp.bfloat16)
    mixed = jnp.dot(normed.reshape(-1, block_shape[-1]), weight, preferred_element_type=jnp.float32)
    return (block_in.astype(jnp.float32) + mixed.reshape(block_shape)).astype(jnp.bfloat16)


def backward_block(cotangent, restored, weight, scale_row):
    block_shape = restored.shape
    standard, inverse = norm_rows(restored.astype(jnp.float32))
    d_normed = lax.dot_general(
        cotangent.reshape(-1, block_shape[-1]),
        weight,
        (((1,), (1,)), ((), ())),
        preferred_element_type=jnp.float32,
    ).reshape(block_shape)
    d_standard = d_normed * scale_row
    d_input = cotangent.astype(jnp.float32) + inverse * (
        d_standard
        - jnp.mean(d_standard, axis=-1, keepdims=True)
        - standard * jnp.mean(d_standard * standard, axis=-1, keepdims=True)
    )
    return d_input.astype(jnp.bfloat16)


def contrastive(logits, label_values):
    count = logits.shape[0]
    targets = (label_values[:, None] == jnp.arange(count).astype(jnp.float32)[None, :]).astype(
        jnp.float32
    )
    row_lse = jax.nn.logsumexp(logits, axis=1)
    col_lse = jax.nn.logsumexp(logits, axis=0)
    picked = jnp.sum(logits * targets, axis=1)
    col_picked = jnp.sum(col_lse[None, :] * targets, axis=1)
    loss_value = 0.5 * jnp.mean(row_lse - picked) + 0.5 * jnp.mean(col_picked - picked)
    row_prob = jnp.exp(logits - row_lse[:, None])
    col_prob = jnp.exp(logits - col_lse[None, :])
    d_logits = 0.5 * (row_prob - targets + (col_prob - targets))
    return (loss_value, d_logits)


def local(
    activations,
    saved,
    cotangents,
    projection,
    section_gain,
    final_gain,
    head_weight,
    text_embed,
    labels,
):
    sections = lax.axis_size("section")
    section_index = lax.axis_index("section")
    is_last = section_index == sections - 1
    weight = projection[0]
    scale_row = section_gain[0]
    incoming = activations[0]
    block_out = forward_block(incoming, weight, scale_row)
    next_act = shifted(block_out[None], "section", 1)
    d_input = backward_block(cotangents[0], saved[0], weight, scale_row)
    passed_grad = shifted(d_input[None], "section", -1)
    pooled = jnp.mean(block_out.astype(jnp.float32), axis=1)
    pooled_std, pooled_inv = norm_rows(pooled)
    pooled_norm = (pooled_std * final_gain).astype(jnp.bfloat16)
    shared = spread(pooled_norm, "section", sections - 1)
    row_count = head_weight.shape[0]
    my_columns = lax.dynamic_slice_in_dim(shared, section_index * row_count, row_count, 1)
    embedding = lax.psum(
        jnp.dot(my_columns, head_weight, preferred_element_type=jnp.float32), "section"
    )
    image_unit, image_inv = unit_rows(embedding)
    own_count = image_unit.shape[0]
    text_unit, text_inv = unit_rows(text_embed.astype(jnp.float32))
    all_image, all_text, all_labels = (
        lax.all_gather(image_unit, "dp", axis=0, tiled=True),
        lax.all_gather(text_unit, "dp", axis=0, tiled=True),
        lax.all_gather(labels.astype(jnp.float32), "dp", axis=0, tiled=True),
    )
    logits = logit_scale * jnp.dot(all_image, all_text.T, precision=lax.Precision.HIGHEST)
    loss_value, d_logits = contrastive(logits, all_labels)
    own_rows = lax.dynamic_slice_in_dim(d_logits, lax.axis_index("dp") * own_count, own_count, 0)
    d_image = logit_scale * jnp.dot(own_rows, all_text, precision=lax.Precision.HIGHEST)
    d_embedding = (
        (d_image - image_unit * jnp.sum(d_image * image_unit, axis=-1, keepdims=True)) * image_inv
    ).astype(jnp.bfloat16)
    partial_value = lax.dot_general(
        d_embedding, head_weight, (((1,), (1,)), ((), ())), preferred_element_type=jnp.float32
    )
    d_pooled_norm = lax.all_gather(partial_value, "section", axis=1, tiled=True)
    d_std = d_pooled_norm * final_gain
    d_pooled = pooled_inv * (
        d_std
        - jnp.mean(d_std, axis=-1, keepdims=True)
        - pooled_std * jnp.mean(d_std * pooled_std, axis=-1, keepdims=True)
    )
    token_count = block_out.shape[1]
    loss_grad = jnp.broadcast_to((d_pooled / token_count)[:, None, :], block_out.shape).astype(
        jnp.bfloat16
    )
    next_grad = jnp.where(is_last, loss_grad[None], passed_grad)
    mean_loss = jnp.where(is_last, loss_value, jnp.float32(0.0))[None]
    return (next_act, next_grad, mean_loss)


def solution(mesh):
    return jax.shard_map(
        local,
        mesh=mesh,
        in_specs=(
            P("section", "dp", None, None),
            P("section", "dp", None, None),
            P("section", "dp", None, None),
            P("section", None, None),
            P("section", None),
            P(),
            P("section", None),
            P("dp", None),
            P("dp"),
        ),
        out_specs=(P("section", "dp", None, None), P("section", "dp", None, None), P("section")),
        check_vma=False,
    )
```

profile of v0, /device:TPU:0, one launch (start us, length us, event | category | flops | bytes accessed | tf_op | source)
XLA Modules:
  0.0 115.6 jit_solution(8883535703884968360)
XLA Ops:
  0.6 0.0 copy-start
  0.6 0.0 copy-start.2
  0.7 1.5 %convert_reduce_fusion = f32[257]{0:T(512)S(1)} fusion(bf16[1,1,257,1792]{3,2,1,0:T(8,128)(2,1)} %param.9), kind=kLoop, calls=%fused_computation.6 | loop fusion | flops 920831 | bytes 922116 | tf_op jit(solution)/shard_map/reduce_sum | solution.py:22
  2.2 1.6 %fusion.30 = f32[257]{0:T(512)S(1)} fusion(bf16[1,1,257,1792]{3,2,1,0:T(8,128)(2,1)} %param.9, f32[257]{0:T(512)S(1)} %broadcast_multiply_fusion.5), kind=kLoop, calls=%fused_computation.31 | loop fusion | flops 1841919 | bytes 923144 | tf_op jit(solution)/shard_map/reduce_sum | solution.py:24
  3.8 0.0 copy-done.6
  3.9 0.0 copy-done.2
  3.9 0.0 copy-start.1
  3.9 5.8 %convert_reduce_fusion.2 = (f32[1792]{0:T(1024)S(1)}, bf16[257,1792]{1,0:T(8,128)(2,1)}) fusion(bf16[1,1792,1792]{2,1,0:T(8,128)(2,1)} %param.12, bf16[1,1,257,1792]{3,2,1,0:T(8,128)(2,1)S(1)} %copy-done.2, f32[1792]{0:T(1024)S(1)} %reduce.23, f32[257]{0:T(512)S(1)} %add_rsqrt_fusion.1, f32[257]{0:T(512)S(1)} %broadcast_multiply_fusion.5), kind=kOutput, calls=%fused_computation.32 | convolution fusion | flops 1655193344 | bytes 8281096 | tf_op jit(solution)/shard_map/dot_general | solution.py:38
  9.7 5.0 %collective-permute-start = (bf16[1,1,257,1792]{3,2,1,0:T(8,128)(2,1)}, bf16[1,1,257,1792]{3,2,1,0:T(8,128)(2,1)S(1)}, u32[]{:S(2)}, u32[]{:S(2)}) collective-permute-start(bf16[1,1,257,1792]{3,2,1,0:T(8,128)(2,1)} %bitcast.4), channel_id=1, source_target_pairs={{0,8},{8,16},{16,24},{1,9},{9,17},{17,25},{2,10},{10,18},{18,26},{... | collective-permute-start | bytes 2763272 | tf_op jit(solution)/shard_map/ppermute | solution.py:13
  14.8 0.2 convert_reduce_fusion.1
  15.0 0.4 fusion.15
  15.4 4.9 %fusion.68 = (f32[257]{0:T(512)S(1)}, f32[257]{0:T(512)S(1)}, f32[257,1792]{1,0:T(8,128)S(1)}) fusion(f32[257]{0:T(512)S(1)} %add_rsqrt_fusion, f32[257]{0:T(512)S(1)} %broadcast_multiply_fusion.4, bf16[1,1,257,1792]{3,2,1,0:T(8,128)(2,1)S(1)} %copy-done.1, f32[1792]{0:T(1024)S(1)} %reduce.23, bf16[1,1792,1792]{2,1,0:T(8,128)(2,1)} %param.12, ...), kind=kOutput, calls=%fused_computation.102 | convolution fusion | flops 1653812992 | bytes 10118160 | tf_op jit(solution)/shard_map/dot_general | solution.py:45
  20.4 0.0 copy-start.5
  20.4 0.0 copy-start.8
  20.4 0.0 copy-start.4
  20.4 0.0 copy-start.7
  20.4 0.8 fusion.33
  21.2 1.3 %collective-permute-start.1 = (bf16[1,1,257,1792]{3,2,1,0:T(8,128)(2,1)S(1)}, bf16[1,1,257,1792]{3,2,1,0:T(8,128)(2,1)}, u32[]{:S(2)}, u32[]{:S(2)}) collective-permute-start(bf16[1,1,257,1792]{3,2,1,0:T(8,128)(2,1)S(1)} %fusion.33), channel_id=1, source_target_pairs={{8,0},{16,8},{24,16},{9,1},{17,9},{25,17},{10,2},{18,10},{26,18},{... | collective-permute-start | bytes 2763272 | tf_op jit(solution)/shard_map/ppermute | solution.py:13
  23.2 0.0 copy-done.5
  23.2 0.6 multiply_reduce_fusion.4
  24.5 0.6 dynamic-slice
  25.1 0.7 convert_dynamic-update-slice_fusion
  25.8 16.4 %all-reduce = f32[8]{0:T(128)S(1)} all-reduce(f32[8]{0:T(128)S(1)} %convert_dynamic-update-slice_fusion), channel_id=1, replica_groups=mesh['section'=4,'dp'=8] {'dp'}, use_global_device_ids=true, to_apply=%add | all-reduce | flops 8 | bytes 64
  42.2 14.1 %all-gather.2 = f32[8,1,1024]{2,1,0:T(1,128)S(1)} all-gather(f32[1,1,1024]{2,1,0:T(1,128)S(1)} %multiply_bitcast_fusion), channel_id=1, replica_groups=mesh['section'=4,'dp'=8] {'dp'}, dimensions={0}, use_global_device_ids=true | all-gather | bytes 36864 | tf_op jit(solution)/shard_map/all_gather | solution.py:111
  56.3 0.6 multiply_reduce_fusion.2
  57.5 0.6 multiply_reduce_fusion.1
  58.9 11.8 %psum.14 = bf16[1,1792]{1,0:T(2,128)(2,1)S(1)} all-reduce(bf16[1,1792]{1,0:T(2,128)(2,1)S(1)} %select_n.52), channel_id=1, replica_groups=mesh['section'=4,'dp'=8] {'section'}, use_global_device_ids=true, to_apply=%region_5.0 | all-reduce | flops 1792 | bytes 7168 | tf_op jit(solution)/shard_map/psum | solution.py:18
  70.7 0.0 copy-done
  70.7 0.3 fusion.58
  70.9 7.9 %psum.15 = f32[1,1024]{1,0:T(1,128)S(1)} all-reduce(f32[1,1024]{1,0:T(1,128)S(1)} %fusion.58), channel_id=1, replica_groups=mesh['section'=4,'dp'=8] {'section'}, use_global_device_ids=true, to_apply=%region_6.0 | all-reduce | flops 1024 | bytes 8192 | tf_op jit(solution)/shard_map/psum | solution.py:103
  78.8 0.6 multiply_reduce_fusion.5
  80.1 14.1 %all-gather.1 = f32[8,1,1024]{2,1,0:T(1,128)S(1)} all-gather(f32[1,1,1024]{2,1,0:T(1,128)S(1)} %fusion.67), channel_id=1, replica_groups=mesh['section'=4,'dp'=8] {'dp'}, dimensions={0}, use_global_device_ids=true | all-gather | bytes 36864 | tf_op jit(solution)/shard_map/all_gather | solution.py:110
  94.2 0.3 fusion.70
  94.5 0.2 fusion.49
  94.8 0.2 fusion.50
  94.9 0.6 subtract_reduce_fusion
  95.6 0.1 fusion.48
  95.6 0.2 fusion.38
  95.8 0.6 dynamic-slice.1
  98.4 0.6 multiply_reduce_fusion.3
  99.0 1.0 fusion.52
  100.0 0.2 dynamic-update-slice.1
  100.2 9.2 %all-reduce.1 = f32[1792]{0:T(1024)S(1)} all-reduce(f32[1792]{0:T(1024)S(1)} %dynamic-update-slice.1), channel_id=2, replica_groups=mesh['section'=4,'dp'=8] {'section'}, use_global_device_ids=true, to_apply=%add.1 | all-reduce | flops 1792 | bytes 14336
  109.4 0.7 fusion.69
  111.4 0.0 collective-permute-done
  111.4 0.0 collective-permute-done.1
  111.4 2.2 %broadcast_select_fusion = bf16[1,1,257,1792]{3,2,1,0:T(8,128)(2,1)} fusion(bf16[1,1,257,1792]{3,2,1,0:T(8,128)(2,1)} %collective-permute-done.1, pred[]{:T(512)S(6)} %eq.8, bf16[1792]{0:T(1024)(128)(2,1)S(1)} %multiply_convert_fusion), kind=kLoop, calls=%fused_computation.40 | loop fusion | flops 460544 | bytes 1845761 | tf_op jit(solution)/shard_map/jit(_where)/select_n | solution.py:135
  113.6 0.9 copy.34
  (24 shorter events, 0.1 us)
Async XLA Ops:
  0.6 70.0 %copy-start = (bf16[448,1024]{1,0:T(8,128)(2,1)S(1)}, bf16[448,1024]{1,0:T(8,128)(2,1)}, u32[]{:S(2)}) copy-start(bf16[448,1024]{1,0:T(8,128)(2,1)} %param.15) | copy-start | bytes 2752516
  0.6 3.2 %copy-start.2 = (bf16[1,1,257,1792]{3,2,1,0:T(8,128)(2,1)S(1)}, bf16[1,1,257,1792]{3,2,1,0:T(8,128)(2,1)}, u32[]{:S(2)}) copy-start(bf16[1,1,257,1792]{3,2,1,0:T(8,128)(2,1)} %param.9) | copy-start | bytes 2763268
  0.7 3.2 %copy-start.6 = (f32[1,1792]{1,0:T(1,128)S(1)}, f32[1,1792]{1,0:T(1,128)}, u32[]{:S(2)}) copy-start(f32[1,1792]{1,0:T(1,128)} %param.13) | copy-start | bytes 21508
  3.9 10.9 %copy-start.1 = (bf16[1,1,257,1792]{3,2,1,0:T(8,128)(2,1)S(1)}, bf16[1,1,257,1792]{3,2,1,0:T(8,128)(2,1)}, u32[]{:S(2)}) copy-start(bf16[1,1,257,1792]{3,2,1,0:T(8,128)(2,1)} %param.10) | copy-start | bytes 2763268
  9.7 5.7 %copy-start.3 = (bf16[1,1,257,1792]{3,2,1,0:T(8,128)(2,1)S(1)}, bf16[1,1,257,1792]{3,2,1,0:T(8,128)(2,1)}, u32[]{:S(2)}) copy-start(bf16[1,1,257,1792]{3,2,1,0:T(8,128)(2,1)} %param.11) | copy-start | bytes 2763268
  9.7 101.7 %collective-permute-start = (bf16[1,1,257,1792]{3,2,1,0:T(8,128)(2,1)}, bf16[1,1,257,1792]{3,2,1,0:T(8,128)(2,1)S(1)}, u32[]{:S(2)}, u32[]{:S(2)}) collective-permute-start(bf16[1,1,257,1792]{3,2,1,0:T(8,128)(2,1)} %bitcast.4), channel_id=1, source_target_pairs={{0,8},{8,16},{16,24},{1,9},{9,17},{17,25},{2,10},{10,18},{18,26},{... | collective-permute-start | bytes 2763272 | tf_op jit(solution)/shard_map/ppermute | solution.py:13
  20.4 2.8 %copy-start.5 = (bf16[1,1024]{1,0:T(2,128)(2,1)S(1)}, bf16[1,1024]{1,0:T(2,128)(2,1)}, u32[]{:S(2)}) copy-start(bf16[1,1024]{1,0:T(2,128)(2,1)} %param.16) | copy-start | bytes 6148
  20.4 4.0 %copy-start.8 = (u32[32]{0:T(128)S(1)}, u32[32]{0:T(128)}, u32[]{:S(2)}) copy-start(u32[32]{0:T(128)} %constant.76) | copy-start | bytes 388
  20.4 38.4 %copy-start.4 = (f32[1792]{0:T(1024)S(1)}, f32[1792]{0:T(1024)}, u32[]{:S(2)}) copy-start(f32[1792]{0:T(1024)} %param.14) | copy-start | bytes 21508
  20.4 75.4 %copy-start.7 = (u32[32]{0:T(128)S(1)}, u32[32]{0:T(128)}, u32[]{:S(2)}) copy-start(u32[32]{0:T(128)} %constant.81) | copy-start | bytes 388
  21.2 90.2 %collective-permute-start.1 = (bf16[1,1,257,1792]{3,2,1,0:T(8,128)(2,1)S(1)}, bf16[1,1,257,1792]{3,2,1,0:T(8,128)(2,1)}, u32[]{:S(2)}, u32[]{:S(2)}) collective-permute-start(bf16[1,1,257,1792]{3,2,1,0:T(8,128)(2,1)S(1)} %fusion.33), channel_id=1, source_target_pairs={{8,0},{16,8},{24,16},{9,1},{17,9},{25,17},{10,2},{18,10},{26,18},{... | collective-permute-start | bytes 2763272 | tf_op jit(solution)/shard_map/ppermute | solution.py:13
where the time goes:
time: 116 us
  blocking collectives  73.4 us (63%)
  matrix products  12.5 us (11%)
  other arithmetic  12.4 us (11%)
  between operations  8.64 us (7%)
  starting transfers between devices  6.34 us (5%)
  local copies, waits for them, and re-layouts  2.44 us (2%)
    unnamed x2, blocking collectives  25.5 us
    all_gather x1, blocking collectives, local(): lax.all_gather(image_unit, 'dp', axis=0, tiled=True)  14.1 us
    all_gather x1, blocking collectives, local(): lax.all_gather(text_unit, 'dp', axis=0, tiled=True)  14.1 us
    psum x1, blocking collectives, spread(): return lax.psum(block, axis)  11.8 us
    psum x1, blocking collectives, local(): lax.psum(jnp.dot(my_columns, head_weight, preferred_element_type=jnp.floa...  7.87 us
    ppermute x2, starting transfers between devices, shifted(): lax.ppermute(value, axis, [(source, source + steps) for source in range(f...  6.34 us
    dot_general x1, matrix products, forward_block(): jnp.dot(normed.reshape(-1, block_shape[-1]), weight, preferred_element_ty...  5.82 us
    dot_general x1, matrix products, backward_block(): lax.dot_general(cotangent.reshape(-1, block_shape[-1]), weight, (((1,), (...  4.94 us
  transfers between devices with their start and end apart: 2, of which 0 were waited for; matrix products, arithmetic and copies ran while one was open for 13% of the time, Pallas kernels for 0%

commit v1 on v0

--- a/solution.py
+++ b/solution.py
@@ -100,9 +100,8 @@
     shared = spread(pooled_norm, "section", sections - 1)
     row_count = head_weight.shape[0]
     my_columns = lax.dynamic_slice_in_dim(shared, section_index * row_count, row_count, 1)
-    embedding = lax.psum(
-        jnp.dot(my_columns, head_weight, preferred_element_type=jnp.float32), "section"
-    )
+    buf = jnp.dot(my_columns, head_weight, preferred_element_type=jnp.float32)
+    embedding = jnp.sum(lax.all_gather(buf, "section"), 0)
     image_unit, image_inv = unit_rows(embedding)
     own_count = image_unit.shape[0]
     text_unit, text_inv = unit_rows(text_embed.astype(jnp.float32))

time: 116 us -> 115 us (level)
    psum x1 -> x0, blocking collectives: 7.87 us -> none  [local(): lax.psum(jnp.dot(my_columns, head_weight, preferred_element_type=jnp.floa...]
    all_gather x0 -> x1, blocking collectives: none -> 7.23 us  [local(): embedding = jnp.sum(lax.all_gather(buf, 'section'), 0)]
where the time goes in v1:
time: 115 us
  blocking collectives  72.6 us (63%)
  other arithmetic  13 us (11%)
  matrix products  11.8 us (10%)
  between operations  8.64 us (8%)
  starting transfers between devices  6.34 us (6%)
  local copies, waits for them, and re-layouts  2.47 us (2%)
    unnamed x2, blocking collectives  25.4 us
    all_gather x1, blocking collectives, local(): lax.all_gather(image_unit, 'dp', axis=0, tiled=True)  14.1 us
    all_gather x1, blocking collectives, local(): lax.all_gather(text_unit, 'dp', axis=0, tiled=True)  14.1 us
    psum x1, blocking collectives, spread(): return lax.psum(block, axis)  11.8 us
    all_gather x1, blocking collectives, local(): embedding = jnp.sum(lax.all_gather(buf, 'section'), 0)  7.23 us
    ppermute x2, starting transfers between devices, shifted(): lax.ppermute(value, axis, [(source, source + steps) for source in range(f...  6.34 us
    dot_general x1, matrix products, forward_block(): jnp.dot(normed.reshape(-1, block_shape[-1]), weight, preferred_element_ty...  5.82 us
    dot_general x1, matrix products, backward_block(): lax.dot_general(cotangent.reshape(-1, block_shape[-1]), weight, (((1,), (...  4.94 us
  transfers between devices with their start and end apart: 2, of which 0 were waited for; matrix products, arithmetic and copies ran while one was open for 13% of the time, Pallas kernels for 0%

profile of v1, /device:TPU:0, one launch (start us, length us, event | category | flops | bytes accessed | tf_op | source)
XLA Modules:
  0.0 114.9 jit_solution(4383267107033923629)
XLA Ops:
  0.6 0.0 copy-start
  0.6 0.0 copy-start.2
  0.7 1.5 %convert_reduce_fusion = f32[257]{0:T(512)S(1)} fusion(bf16[1,1,257,1792]{3,2,1,0:T(8,128)(2,1)} %param.9), kind=kLoop, calls=%fused_computation.6 | loop fusion | flops 920831 | bytes 922116 | tf_op jit(solution)/shard_map/reduce_sum | solution.py:22
  2.2 1.6 %fusion.30 = f32[257]{0:T(512)S(1)} fusion(bf16[1,1,257,1792]{3,2,1,0:T(8,128)(2,1)} %param.9, f32[257]{0:T(512)S(1)} %broadcast_multiply_fusion.4), kind=kLoop, calls=%fused_computation.31 | loop fusion | flops 1841919 | bytes 923144 | tf_op jit(solution)/shard_map/reduce_sum | solution.py:24
  3.8 0.0 copy-done.6
  3.9 0.0 copy-done.2
  3.9 0.0 copy-start.1
  3.9 5.8 %convert_reduce_fusion.2 = (f32[1792]{0:T(1024)S(1)}, bf16[257,1792]{1,0:T(8,128)(2,1)}) fusion(bf16[1,1792,1792]{2,1,0:T(8,128)(2,1)} %param.12, bf16[1,1,257,1792]{3,2,1,0:T(8,128)(2,1)S(1)} %copy-done.2, f32[1792]{0:T(1024)S(1)} %reduce.27, f32[257]{0:T(512)S(1)} %add_rsqrt_fusion.1, f32[257]{0:T(512)S(1)} %broadcast_multiply_fusion.4), kind=kOutput, calls=%fused_computation.32 | convolution fusion | flops 1655193344 | bytes 8281096 | tf_op jit(solution)/shard_map/dot_general | solution.py:38
  9.7 5.0 %collective-permute-start = (bf16[1,1,257,1792]{3,2,1,0:T(8,128)(2,1)}, bf16[1,1,257,1792]{3,2,1,0:T(8,128)(2,1)S(1)}, u32[]{:S(2)}, u32[]{:S(2)}) collective-permute-start(bf16[1,1,257,1792]{3,2,1,0:T(8,128)(2,1)} %bitcast.4), channel_id=1, source_target_pairs={{0,8},{8,16},{16,24},{1,9},{9,17},{17,25},{2,10},{10,18},{18,26},{... | collective-permute-start | bytes 2763272 | tf_op jit(solution)/shard_map/ppermute | solution.py:13
  14.8 0.2 convert_reduce_fusion.1
  15.0 0.4 fusion.15
  15.4 4.9 %fusion.57 = (f32[257]{0:T(512)S(1)}, f32[257]{0:T(512)S(1)}, f32[257,1792]{1,0:T(8,128)S(1)}) fusion(f32[257]{0:T(512)S(1)} %add_rsqrt_fusion, f32[257]{0:T(512)S(1)} %broadcast_multiply_fusion.3, bf16[1,1,257,1792]{3,2,1,0:T(8,128)(2,1)S(1)} %copy-done.1, f32[1792]{0:T(1024)S(1)} %reduce.27, bf16[1,1792,1792]{2,1,0:T(8,128)(2,1)} %param.12, ...), kind=kOutput, calls=%fused_computation.91 | convolution fusion | flops 1653812992 | bytes 10118160 | tf_op jit(solution)/shard_map/dot_general | solution.py:45
  20.4 0.0 copy-start.5
  20.4 0.0 copy-start.8
  20.4 0.0 copy-start.7
  20.4 0.0 copy-start.4
  20.4 0.8 fusion.33
  21.2 1.3 %collective-permute-start.1 = (bf16[1,1,257,1792]{3,2,1,0:T(8,128)(2,1)S(1)}, bf16[1,1,257,1792]{3,2,1,0:T(8,128)(2,1)}, u32[]{:S(2)}, u32[]{:S(2)}) collective-permute-start(bf16[1,1,257,1792]{3,2,1,0:T(8,128)(2,1)S(1)} %fusion.33), channel_id=1, source_target_pairs={{8,0},{16,8},{24,16},{9,1},{17,9},{25,17},{10,2},{18,10},{26,18},{... | collective-permute-start | bytes 2763272 | tf_op jit(solution)/shard_map/ppermute | solution.py:13
  23.2 0.0 copy-done.5
  23.2 0.6 multiply_reduce_fusion.4
  24.5 0.6 dynamic-slice
  25.1 0.7 convert_dynamic-update-slice_fusion
  25.8 0.6 dynamic-slice.1
  26.5 16.3 %all-reduce = f32[8]{0:T(128)S(1)} all-reduce(f32[8]{0:T(128)S(1)} %convert_dynamic-update-slice_fusion), channel_id=1, replica_groups=mesh['section'=4,'dp'=8] {'dp'}, use_global_device_ids=true, to_apply=%add | all-reduce | flops 8 | bytes 64
  42.8 14.1 %all-gather.3 = f32[8,1,1024]{2,1,0:T(1,128)S(1)} all-gather(f32[1,1,1024]{2,1,0:T(1,128)S(1)} %multiply_bitcast_fusion), channel_id=1, replica_groups=mesh['section'=4,'dp'=8] {'dp'}, dimensions={0}, use_global_device_ids=true | all-gather | bytes 36864 | tf_op jit(solution)/shard_map/all_gather | solution.py:110
  56.9 0.6 multiply_reduce_fusion.2
  58.2 0.6 multiply_reduce_fusion.1
  59.5 11.8 %psum.7 = bf16[1,1792]{1,0:T(2,128)(2,1)S(1)} all-reduce(bf16[1,1792]{1,0:T(2,128)(2,1)S(1)} %select_n.52), channel_id=1, replica_groups=mesh['section'=4,'dp'=8] {'section'}, use_global_device_ids=true, to_apply=%region_5.0 | all-reduce | flops 1792 | bytes 7168 | tf_op jit(solution)/shard_map/psum | solution.py:18
  71.3 0.3 fusion.50
  71.6 7.2 %all-gather = f32[4096]{0:T(1024)S(1)} all-gather(f32[1024]{0:T(1024)S(1)} %bitcast.99), channel_id=2, replica_groups=mesh['section'=4,'dp'=8] {'section'}, dimensions={0}, use_global_device_ids=true | all-gather | bytes 20480 | tf_op jit(solution)/shard_map/all_gather | solution.py:104
  78.8 0.6 multiply_reduce_fusion.5
  80.1 14.1 %all-gather.1 = f32[8192]{0:T(1024)S(1)} all-gather(f32[1024]{0:T(1024)S(1)} %broadcast_multiply_fusion), channel_id=3, replica_groups=mesh['section'=4,'dp'=8] {'dp'}, dimensions={0}, use_global_device_ids=true | all-gather | bytes 36864 | tf_op jit(solution)/shard_map/all_gather | solution.py:109
  94.2 0.3 fusion.59
  94.5 0.2 fusion.47
  94.8 0.2 fusion.48
  95.0 0.6 subtract_reduce_fusion
  96.9 0.1 fusion.46
  97.0 0.2 fusion.38
  97.1 0.6 multiply_reduce_fusion.3
  97.7 0.7 multiply_convert_fusion.2
  99.0 0.4 fusion.60
  99.4 0.2 dynamic-update-slice.1
  99.6 9.1 %all-reduce.1 = f32[1792]{0:T(1024)S(1)} all-reduce(f32[1792]{0:T(1024)S(1)} %dynamic-update-slice.1), channel_id=4, replica_groups=mesh['section'=4,'dp'=8] {'section'}, use_global_device_ids=true, to_apply=%add.1 | all-reduce | flops 1792 | bytes 14336
  108.7 0.7 fusion.58
  110.6 0.0 collective-permute-done
  110.6 0.0 collective-permute-done.1
  110.6 2.2 %broadcast_select_fusion = bf16[1,1,257,1792]{3,2,1,0:T(8,128)(2,1)} fusion(bf16[1,1,257,1792]{3,2,1,0:T(8,128)(2,1)} %collective-permute-done.1, pred[]{:T(512)S(6)} %eq.8, bf16[1792]{0:T(1024)(128)(2,1)S(1)} %multiply_convert_fusion), kind=kLoop, calls=%fused_computation.40 | loop fusion | flops 460544 | bytes 1845761 | tf_op jit(solution)/shard_map/jit(_where)/select_n | solution.py:134
  112.8 0.9 copy.27
  (28 shorter events, 0.2 us)
Async XLA Ops:
  0.6 70.7 %copy-start = (bf16[448,1024]{1,0:T(8,128)(2,1)S(1)}, bf16[448,1024]{1,0:T(8,128)(2,1)}, u32[]{:S(2)}) copy-start(bf16[448,1024]{1,0:T(8,128)(2,1)} %param.15) | copy-start | bytes 2752516
  0.6 3.2 %copy-start.2 = (bf16[1,1,257,1792]{3,2,1,0:T(8,128)(2,1)S(1)}, bf16[1,1,257,1792]{3,2,1,0:T(8,128)(2,1)}, u32[]{:S(2)}) copy-start(bf16[1,1,257,1792]{3,2,1,0:T(8,128)(2,1)} %param.9) | copy-start | bytes 2763268
  0.7 3.2 %copy-start.6 = (f32[1,1792]{1,0:T(1,128)S(1)}, f32[1,1792]{1,0:T(1,128)}, u32[]{:S(2)}) copy-start(f32[1,1792]{1,0:T(1,128)} %param.13) | copy-start | bytes 21508
  3.9 10.9 %copy-start.1 = (bf16[1,1,257,1792]{3,2,1,0:T(8,128)(2,1)S(1)}, bf16[1,1,257,1792]{3,2,1,0:T(8,128)(2,1)}, u32[]{:S(2)}) copy-start(bf16[1,1,257,1792]{3,2,1,0:T(8,128)(2,1)} %param.10) | copy-start | bytes 2763268
  9.7 5.7 %copy-start.3 = (bf16[1,1,257,1792]{3,2,1,0:T(8,128)(2,1)S(1)}, bf16[1,1,257,1792]{3,2,1,0:T(8,128)(2,1)}, u32[]{:S(2)}) copy-start(bf16[1,1,257,1792]{3,2,1,0:T(8,128)(2,1)} %param.11) | copy-start | bytes 2763268
  9.7 100.9 %collective-permute-start = (bf16[1,1,257,1792]{3,2,1,0:T(8,128)(2,1)}, bf16[1,1,257,1792]{3,2,1,0:T(8,128)(2,1)S(1)}, u32[]{:S(2)}, u32[]{:S(2)}) collective-permute-start(bf16[1,1,257,1792]{3,2,1,0:T(8,128)(2,1)} %bitcast.4), channel_id=1, source_target_pairs={{0,8},{8,16},{16,24},{1,9},{9,17},{17,25},{2,10},{10,18},{18,26},{... | collective-permute-start | bytes 2763272 | tf_op jit(solution)/shard_map/ppermute | solution.py:13
  20.4 2.8 %copy-start.5 = (bf16[1,1024]{1,0:T(2,128)(2,1)S(1)}, bf16[1,1024]{1,0:T(2,128)(2,1)}, u32[]{:S(2)}) copy-start(bf16[1,1024]{1,0:T(2,128)(2,1)} %param.16) | copy-start | bytes 6148
  20.4 4.1 %copy-start.8 = (u32[32]{0:T(128)S(1)}, u32[32]{0:T(128)}, u32[]{:S(2)}) copy-start(u32[32]{0:T(128)} %constant.76) | copy-start | bytes 388
  20.4 5.4 %copy-start.7 = (u32[32]{0:T(128)S(1)}, u32[32]{0:T(128)}, u32[]{:S(2)}) copy-start(u32[32]{0:T(128)} %constant.81) | copy-start | bytes 388
  20.4 39.0 %copy-start.4 = (f32[1792]{0:T(1024)S(1)}, f32[1792]{0:T(1024)}, u32[]{:S(2)}) copy-start(f32[1792]{0:T(1024)} %param.14) | copy-start | bytes 21508
  21.2 89.4 %collective-permute-start.1 = (bf16[1,1,257,1792]{3,2,1,0:T(8,128)(2,1)S(1)}, bf16[1,1,257,1792]{3,2,1,0:T(8,128)(2,1)}, u32[]{:S(2)}, u32[]{:S(2)}) collective-permute-start(bf16[1,1,257,1792]{3,2,1,0:T(8,128)(2,1)S(1)} %fusion.33), channel_id=1, source_target_pairs={{8,0},{16,8},{24,16},{9,1},{17,9},{25,17},{10,2},{18,10},{26,18},{... | collective-permute-start | bytes 2763272 | tf_op jit(solution)/shard_map/ppermute | solution.py:13
